TPU v7x, 32 devices: a whole 2x2x4 slice. The times are simulated.
32 devices in a mesh: tab: 8 (over z, x), rep: 4 (over y, core).
Axes of the slice: x: 2, y: 2, z: 4, core: 2. Of those that a mesh axis runs over, the one named last changes fastest.
Arguments:
- sample_ids: int32 [16384, 26], P(('tab', 'rep')), may hold values from 0 to 4095, as said below
- features: bfloat16 [16384, 27, 128], P(('tab', 'rep')), may hold values from -6 to 6
- pair_grad: bfloat16 [351, 16384], P(None, ('tab', 'rep')), may hold values from -1.59375 to 1.59375
Outputs:
- table_grad: float32 [26, 4096, 128], P(None, ('tab', 'rep'))
- dense_grad: float32 [16384, 128], P(('tab', 'rep'))
Inputs may be any that keep to these rules, and one draw needn't show every extreme that they name: `sample_ids`: row r is owned by device r // 128, numbered tab * 4 + rep. For each field and the 512 samples of one device (aligned blocks of rows in device order), at most 32 ids fall in the rows of any one device, and at most 128 in the rows of any one tab index; in every block and field both bounds are reached.
All inputs are finite; a program needn't handle non-finite values.
Results may differ from a plain program's by a relative error of at most 0.0029.
Values may be sent and summed in bfloat16 or wider, within the bound.
No kernel may reach another device: no remote copies, remote signals or barrier semaphores. Data moves between devices by JAX's collectives and lax.ppermute only.
A program may use at most 128 MiB of HBM per device.

v0:
```python
import jax
import jax.numpy as jnp
import numpy as np
from jax import lax
from jax.sharding import PartitionSpec as P

RQ = 128


def pair_table(vectors):
    row_of, col_of = np.tril_indices(vectors, -1)
    spread = np.zeros((row_of.shape[0], vectors * vectors), np.float32)
    places = np.arange(row_of.shape[0])
    spread[places, row_of * vectors + col_of] = 1.0
    spread[places, col_of * vectors + row_of] = 1.0
    return spread


def arrival_order(targets, bins):
    matches = (targets[:, None] == jnp.arange(bins, dtype=jnp.int32)[None, :]).astype(jnp.int32)
    return jnp.sum(jnp.cumsum(matches, axis=0) * matches, axis=1) - 1


def place_field(slot_of, tag_of, grads, slot_total):
    placing = jnp.arange(slot_total, dtype=jnp.int32)[:, None] == slot_of[None, :]
    placed = jnp.dot(
        placing.astype(jnp.bfloat16), grads, preferred_element_type=jnp.float32
    ).astype(jnp.bfloat16)
    shifted = (tag_of + 1).astype(jnp.float32)
    tag_sum = jnp.dot(placing.astype(jnp.float32), shifted, precision=lax.Precision.HIGHEST)
    return (placed, tag_sum.astype(jnp.int32) - 1)


def tally_rows(arrived, row_tags, row_count):

    def per_field(pieces):
        slot_grads, slot_tags = pieces
        matches = (slot_tags[None, :] == jnp.arange(row_count, dtype=jnp.int32)[:, None]).astype(
            jnp.bfloat16
        )
        return jnp.dot(matches, slot_grads, preferred_element_type=jnp.float32)

    return lax.map(per_field, (arrived, row_tags))


def local(sample_ids, features, pair_grad):
    vectors = features.shape[1]
    samples = features.shape[0]
    depth = features.shape[2]
    spread = jnp.asarray(pair_table(vectors).T).astype(jnp.bfloat16)
    symmetric = jnp.dot(spread, pair_grad, preferred_element_type=jnp.float32)
    symmetric = symmetric.astype(jnp.bfloat16).reshape(vectors, vectors, samples)
    gradients = jnp.einsum("fgb,bge->fbe", symmetric, features, preferred_element_type=jnp.float32)
    dense_grad = gradients[0]
    field_grads = gradients[1:].astype(jnp.bfloat16)
    fields = vectors - 1
    col_count = lax.axis_size("tab")
    rep_count = lax.axis_size("rep")
    capacity = 2 * samples // (col_count * rep_count)
    slot_total = col_count * rep_count * capacity
    ids_by_field = sample_ids.T

    def build_owner(pieces):
        column_ids, grads = pieces
        owners = column_ids // RQ
        slot_of = owners * capacity + arrival_order(owners, col_count * rep_count)
        return place_field(slot_of, column_ids % RQ, grads, slot_total)

    outgoing, row_tags = lax.map(build_owner, (ids_by_field, field_grads))
    outgoing = outgoing.reshape(fields, col_count, rep_count, capacity, depth)
    row_tags = row_tags.reshape(fields, col_count, rep_count, capacity)
    arrived, tags_in = (
        lax.all_to_all(
            lax.all_to_all(outgoing, "tab", split_axis=1, concat_axis=1, tiled=True),
            "rep",
            split_axis=2,
            concat_axis=2,
            tiled=True,
        ),
        lax.all_to_all(
            lax.all_to_all(row_tags, "tab", split_axis=1, concat_axis=1, tiled=True),
            "rep",
            split_axis=2,
            concat_axis=2,
            tiled=True,
        ),
    )
    table_grad = tally_rows(arrived.reshape(fields, -1, depth), tags_in.reshape(fields, -1), RQ)
    return (table_grad, dense_grad)


def solution(mesh):
    placed = (P(("tab", "rep"), None), P(("tab", "rep"), None, None), P(None, ("tab", "rep")))
    return jax.shard_map(
        local,
        mesh=mesh,
        in_specs=placed,
        out_specs=(P(None, ("tab", "rep"), None), P(("tab", "rep"), None)),
        check_vma=False,
    )
```

profile of v0, /device:TPU:0, one launch (start us, length us, event | category | flops | bytes accessed | tf_op | source)
XLA Modules:
  0.0 536.2 jit_solution(541020844716352694)
XLA Ops:
  0.7 2.7 convolution_convert_fusion
  3.4 2.2 reshape.112
  5.6 7.5 %copy.20 = bf16[27,27,512]{1,0,2:T(8,128)(2,1)} copy(bf16[27,27,512]{2,1,0:T(8,128)(2,1)} %reshape.112) | data formatting | bytes 1492992 | tf_op jit(solution)/shard_map/reshape | solution.py:52
  13.1 4.5 fusion.25
  18.8 2.1 copy-done.2
  22.2 173.3 %while.25 = (s32[]{:T(128)}, bf16[26,1024,128]{2,1,0:T(8,128)(2,1)}, s32[26,1024]{1,0:T(8,128)}, s32[26,512]{1,0:T(8,128)}, bf16[26,512,128]{2,1,0:T(8,128)(2,1)S(1)}, /*index=5*/s32[]{:T(128)}, s32[]{:T(128)}) while((s32[]{:T(128)}, bf16[26,1024,128]{2,1,0:T(8,128)(2,1)}, s32[26,1024]{1,0:T(8,128)}, s32[26,512]{1,0:T(8,128)}, ...), condition=%wide.region_4.5_spmd, body=%wide.region_0.4_spmd.sunk | while | flops 143897568 | bytes 717545 | solution.py:69
  197.7 7.2 %all-to-all-start = ((s32[8,1,3328]{2,1,0:T(1,128)}), s32[8,1,3328]{2,1,0:T(1,128)S(1)}, u32[]{:S(2)}, u32[]{:S(2)}) async-start(s32[8,1,3328]{2,1,0:T(1,128)} %reshape.120), calls=%async_computation | async-start | bytes 212992 | tf_op jit(solution)/shard_map/all_to_all | solution.py:81
  205.0 8.6 %copy.26 = bf16[26,8,4,32,128]{4,3,2,0,1:T(8,128)(2,1)} copy(bf16[26,8,4,32,128]{4,3,2,1,0:T(8,128)(2,1)} %bitcast.88) | data formatting | bytes 13631488 | tf_op jit(solution)/shard_map/reshape | solution.py:70
  213.6 6.0 %all-to-all-start.2 = ((bf16[26,8,4,32,128]{4,3,2,0,1:T(8,128)(2,1)}), bf16[26,8,4,32,128]{4,3,2,0,1:T(8,128)(2,1)}, u32[]{:S(2)}, u32[]{:S(2)}) async-start(bf16[26,8,4,32,128]{4,3,2,0,1:T(8,128)(2,1)} %copy.26), calls=%async_computation.2 | async-start | bytes 13631488 | tf_op jit(solution)/shard_map/all_to_all | solution.py:74
  222.2 146.3 %all-to-all-done.2 = bf16[26,8,4,32,128]{4,3,2,0,1:T(8,128)(2,1)} async-done(((bf16[26,8,4,32,128]{4,3,2,0,1:T(8,128)(2,1)}), bf16[26,8,4,32,128]{4,3,2,0,1:T(8,128)(2,1)}, u32[]{:S(2)}, u32[]{:S(2)}) %all-to-all-start.2) | async-done | bytes 6815776 | tf_op jit(solution)/shard_map/all_to_all | solution.py:74
  368.5 3.5 all-to-all-start.1
  372.0 7.9 %copy.27 = bf16[26,8,4,32,128]{4,3,1,0,2:T(8,128)(2,1)} copy(bf16[26,8,4,32,128]{4,3,2,0,1:T(8,128)(2,1)} %all-to-all-done.2) | data formatting | bytes 13631488 | tf_op jit(solution)/shard_map/all_to_all | solution.py:74
  379.8 5.4 %all-to-all-start.3 = ((bf16[26,8,4,32,128]{4,3,1,0,2:T(8,128)(2,1)}), bf16[26,8,4,32,128]{4,3,1,0,2:T(8,128)(2,1)}, u32[]{:S(2)}, u32[]{:S(2)}) async-start(bf16[26,8,4,32,128]{4,3,1,0,2:T(8,128)(2,1)} %copy.27), calls=%async_computation.3 | async-start | bytes 13631488 | tf_op jit(solution)/shard_map/all_to_all | solution.py:73
  385.3 2.4 slice.25
  389.9 71.6 %all-to-all-done.3 = bf16[26,8,4,32,128]{4,3,1,0,2:T(8,128)(2,1)} async-done(((bf16[26,8,4,32,128]{4,3,1,0,2:T(8,128)(2,1)}), bf16[26,8,4,32,128]{4,3,1,0,2:T(8,128)(2,1)}, u32[]{:S(2)}, u32[]{:S(2)}) %all-to-all-start.3) | async-done | bytes 6815776 | tf_op jit(solution)/shard_map/all_to_all | solution.py:73
  461.6 8.0 %copy.28 = bf16[26,8,4,32,128]{4,3,2,1,0:T(8,128)(2,1)} copy(bf16[26,8,4,32,128]{4,3,1,0,2:T(8,128)(2,1)} %all-to-all-done.3) | data formatting | bytes 13631488 | tf_op jit(solution)/shard_map/all_to_all | solution.py:73
  469.6 66.7 %while.26 = (s32[]{:T(128)}, f32[26,128,128]{2,1,0:T(8,128)}, s32[26,1024]{1,0:T(8,128)}, bf16[26,1024,128]{2,1,0:T(8,128)(2,1)}, s32[]{:T(128)}) while((s32[]{:T(128)}, f32[26,128,128]{2,1,0:T(8,128)}, s32[26,1024]{1,0:T(8,128)}, bf16[26,1024,128]{2,1,0:T(8,128)(2,1)}, s32[]{:T(128)}) %tuple.59), condition=%wide.region_6.7_spmd, body=%wide.region_5.6_spmd.sunk | while | flops 33685504 | bytes 341065 | solution.py:43
  470.3 1.8 fusion.49
  472.9 1.8 fusion.49
  480.6 1.8 fusion.49
  483.1 1.8 fusion.49
  485.7 1.8 fusion.49
  490.8 1.8 fusion.49
  493.4 1.8 fusion.49
  501.1 1.8 fusion.49
  503.7 1.8 fusion.49
  506.2 1.8 fusion.49
  511.3 1.8 fusion.49
  521.6 1.8 fusion.49
  524.2 1.8 fusion.49
  526.7 1.8 fusion.49
  531.9 1.8 fusion.49
  (451 shorter events, 221.7 us)
Async XLA Ops:
  0.6 12.5 %copy-start = (bf16[512,27,128]{2,0,1:T(8,128)(2,1)S(1)}, bf16[512,27,128]{2,0,1:T(8,128)(2,1)}, u32[]{:S(2)}) copy-start(bf16[512,27,128]{2,0,1:T(8,128)(2,1)} %param.9) | copy-start | bytes 10616836
  17.7 3.2 copy-start.2
  197.7 15.9 %all-to-all-start = ((s32[8,1,3328]{2,1,0:T(1,128)}), s32[8,1,3328]{2,1,0:T(1,128)S(1)}, u32[]{:S(2)}, u32[]{:S(2)}) async-start(s32[8,1,3328]{2,1,0:T(1,128)} %reshape.120), calls=%async_computation | async-start | bytes 212992 | tf_op jit(solution)/shard_map/all_to_all | solution.py:81
  213.6 154.9 %all-to-all-start.2 = ((bf16[26,8,4,32,128]{4,3,2,0,1:T(8,128)(2,1)}), bf16[26,8,4,32,128]{4,3,2,0,1:T(8,128)(2,1)}, u32[]{:S(2)}, u32[]{:S(2)}) async-start(bf16[26,8,4,32,128]{4,3,2,0,1:T(8,128)(2,1)} %copy.26), calls=%async_computation.2 | async-start | bytes 13631488 | tf_op jit(solution)/shard_map/all_to_all | solution.py:74
  368.5 11.4 %all-to-all-start.1 = ((s32[4,1,6656]{2,1,0:T(1,128)}), s32[4,1,6656]{2,1,0:T(1,128)S(1)}, u32[]{:S(2)}, u32[]{:S(2)}) async-start(s32[4,1,6656]{2,1,0:T(1,128)} %reshape.122), calls=%async_computation.1 | async-start | bytes 212992 | tf_op jit(solution)/shard_map/all_to_all | solution.py:80
  379.8 81.7 %all-to-all-start.3 = ((bf16[26,8,4,32,128]{4,3,1,0,2:T(8,128)(2,1)}), bf16[26,8,4,32,128]{4,3,1,0,2:T(8,128)(2,1)}, u32[]{:S(2)}, u32[]{:S(2)}) async-start(bf16[26,8,4,32,128]{4,3,1,0,2:T(8,128)(2,1)} %copy.27), calls=%async_computation.3 | async-start | bytes 13631488 | tf_op jit(solution)/shard_map/all_to_all | solution.py:73
  461.5 74.7 %copy-start.1 = (bf16[512,27,128]{2,0,1:T(8,128)(2,1)S(1)}, bf16[512,27,128]{2,0,1:T(8,128)(2,1)}, u32[]{:S(2)}) copy-start(bf16[512,27,128]{2,0,1:T(8,128)(2,1)} %param.9) | copy-start | bytes 10616836
where the time goes:
time: 544 us; the launch traced here: 536 us
  waiting for transfers between devices  218 us (40%)
  local copies, waits for them, and re-layouts  128 us (24%)
  matrix products  111 us (20%)
  other arithmetic  56.4 us (10%)
  starting transfers between devices  22.1 us (4%)
    all_to_all x1, waiting for transfers between devices, local(): lax.all_to_all(outgoing, 'tab', split_axis=1, concat_axis=1, tiled=True)  146 us
    all_to_all x1, waiting for transfers between devices, local(): lax.all_to_all(lax.all_to_all(outgoing, 'tab', split_axis=1, concat_axis=...  71.6 us
    dot_general x26, matrix products, per_field(): return jnp.dot(matches, slot_grads, preferred_element_type=jnp.float32)  46.8 us
    dynamic_update_slice x26, local copies, waits for them, and re-layouts, local(): outgoing, row_tags = lax.map(build_owner, (ids_by_field, field_grads))  36.6 us
    another operation x52, other arithmetic  31.3 us
    dot_general x26, matrix products, place_field(): jnp.dot(placing.astype(jnp.bfloat16), grads, preferred_element_type=jnp.f...  30.5 us
    dot_general x26, matrix products, place_field(): jnp.dot(placing.astype(jnp.float32), shifted, precision=lax.Precision.HIG...  26.3 us
    dynamic_slice x26, local copies, waits for them, and re-layouts, tally_rows(): return lax.map(per_field, (arrived, row_tags))  19.9 us
  transfers between devices with their start and end apart: 4, of which 2 were waited for; matrix products, arithmetic and copies ran while one was open for 4% of the time, Pallas kernels for 0%

commit v1 on v0

--- a/solution.py
+++ b/solution.py
@@ -5,6 +5,22 @@
 from jax.sharding import PartitionSpec as P
 
 RQ = 128
+
+
+def swapped_with_each(x, axis, split, join):
+    ways, here = (lax.axis_size(axis), lax.axis_index(axis))
+    width = x.shape[split] // ways
+    lengths = list(x.shape)
+    lengths[split] = width
+    height = lengths[join]
+    lengths[join] = height * ways
+    full = jnp.zeros(lengths, x.dtype)
+    for mask in range(ways):
+        part = lax.dynamic_slice_in_dim(x, (here ^ mask) * width, width, axis=split)
+        if mask:
+            part = lax.ppermute(part, axis, [(d, d ^ mask) for d in range(ways)])
+        full = lax.dynamic_update_slice_in_dim(full, part, (here ^ mask) * height, axis=join)
+    return full
 
 
 def pair_table(vectors):
@@ -71,11 +87,7 @@
     row_tags = row_tags.reshape(fields, col_count, rep_count, capacity)
     arrived, tags_in = (
         lax.all_to_all(
-            lax.all_to_all(outgoing, "tab", split_axis=1, concat_axis=1, tiled=True),
-            "rep",
-            split_axis=2,
-            concat_axis=2,
-            tiled=True,
+            swapped_with_each(outgoing, "tab", 1, 1), "rep", split_axis=2, concat_axis=2, tiled=True
         ),
         lax.all_to_all(
             lax.all_to_all(row_tags, "tab", split_axis=1, concat_axis=1, tiled=True),

time: 544 us -> 537 us (0.987)
  the two profiles are of different devices: /device:TPU:0 before, /device:TPU:8 now
where the time goes in v1:
time: 537 us; the launch traced here: 529 us
  waiting for transfers between devices  195 us (36%)
  local copies, waits for them, and re-layouts  137 us (26%)
  matrix products  111 us (21%)
  other arithmetic  56.5 us (11%)
  starting transfers between devices  28.5 us (5%)
    ppermute x7, waiting for transfers between devices, swapped_with_each(): part = lax.ppermute(part, axis, [(d, d ^ mask) for d in range(ways)])  77.2 us
    all_to_all x1, waiting for transfers between devices, local(): lax.all_to_all(swapped_with_each(outgoing, 'tab', 1, 1), 'rep', split_axi...  69.6 us
    all_to_all x1, waiting for transfers between devices, local(): lax.all_to_all(row_tags, 'tab', split_axis=1, concat_axis=1, tiled=True)  48.3 us
    dot_general x26, matrix products, per_field(): return jnp.dot(matches, slot_grads, preferred_element_type=jnp.float32)  46.8 us
    dynamic_update_slice x26, local copies, waits for them, and re-layouts, local(): outgoing, row_tags = lax.map(build_owner, (ids_by_field, field_grads))  36.6 us
    another operation x52, other arithmetic  31.3 us
    dot_general x26, matrix products, place_field(): jnp.dot(placing.astype(jnp.bfloat16), grads, preferred_element_type=jnp.f...  30.3 us
    dot_general x26, matrix products, place_field(): jnp.dot(placing.astype(jnp.float32), shifted, precision=lax.Precision.HIG...  26.3 us
  transfers between devices with their start and end apart: 10, of which 5 were waited for; matrix products, arithmetic and copies ran while one was open for 6% of the time, Pallas kernels for 0%

profile of v1, /device:TPU:8, one launch (start us, length us, event | category | flops | bytes accessed | tf_op | source)
XLA Modules:
  0.0 529.1 jit_solution(14974358607876683724)
XLA Ops:
  0.7 2.7 convolution_convert_fusion
  3.4 2.2 reshape.112
  5.6 7.5 %copy.19 = bf16[27,27,512]{1,0,2:T(8,128)(2,1)} copy(bf16[27,27,512]{2,1,0:T(8,128)(2,1)} %reshape.112) | data formatting | bytes 1492992 | tf_op jit(solution)/shard_map/reshape | solution.py:68
  13.2 4.5 fusion.25
  20.9 173.2 %while.25 = (s32[]{:T(128)}, bf16[26,1024,128]{2,1,0:T(8,128)(2,1)}, s32[26,1024]{1,0:T(8,128)}, s32[26,512]{1,0:T(8,128)}, bf16[26,512,128]{2,1,0:T(8,128)(2,1)S(1)}, /*index=5*/s32[]{:T(128)}, s32[]{:T(128)}) while((s32[]{:T(128)}, bf16[26,1024,128]{2,1,0:T(8,128)(2,1)}, s32[26,1024]{1,0:T(8,128)}, s32[26,512]{1,0:T(8,128)}, ...), condition=%wide.region_4.5_spmd, body=%wide.region_0.4_spmd.sunk | while | flops 143897568 | bytes 717545 | solution.py:85
  194.1 6.7 %constant_dynamic-slice_fusion.2 = (bf16[26,1,4,32,128]{4,3,2,1,0:T(8,128)(2,1)S(1)}, bf16[26,1,4,32,128]{4,3,2,1,0:T(8,128)(2,1)S(1)}, bf16[26,1,4,32,128]{4,3,...) fusion(bf16[26,8,4,32,128]{4,3,2,1,0:T(8,128)(2,1)} %bitcast.87, ...), kind=kLoop, calls=%fused_computation.65 | loop fusion | bytes 13631520 | tf_op jit(solution)/shard_map/dynamic_slice | solution.py:19
  205.5 6.4 %all-to-all-start = ((s32[8,1,3328]{2,1,0:T(1,128)}), s32[8,1,3328]{2,1,0:T(1,128)S(1)}, u32[]{:S(2)}, u32[]{:S(2)}) async-start(s32[8,1,3328]{2,1,0:T(1,128)} %reshape.120), calls=%async_computation | async-start | bytes 212992 | tf_op jit(solution)/shard_map/all_to_all | solution.py:93
  211.9 2.4 collective-permute-start.6
  215.7 4.5 broadcast_in_dim.41
  221.4 48.3 %all-to-all-done = s32[8,1,3328]{2,1,0:T(1,128)S(1)} async-done(((s32[8,1,3328]{2,1,0:T(1,128)}), s32[8,1,3328]{2,1,0:T(1,128)S(1)}, u32[]{:S(2)}, u32[]{:S(2)}) %all-to-all-start) | async-done | bytes 106528 | tf_op jit(solution)/shard_map/all_to_all | solution.py:93
  272.4 3.3 all-to-all-start.1
  275.7 6.2 %collective-permute-start.4 = (bf16[26,1,4,32,128]{4,3,2,1,0:T(8,128)(2,1)S(1)}, bf16[26,1,4,32,128]{4,3,2,1,0:T(8,128)(2,1)S(1)}, u32[]{:S(2)}, u32[]{:S(2)}) collective-permute-start(bf16[26,1,4,32,128]{4,3,2,1,0:T(8,128)(2,1)S(1)} %copy-done.3), channel_id=1, source_target_pairs={{0,20},{4,16},{8,28},{12,24},{16,4},{20,0},{24,12},{28,8},{1,21},{... | collective-permute-start | bytes 2555912 | tf_op jit(solution)/shard_map/ppermute | solution.py:21
  281.9 2.3 copy_dynamic-update-slice_fusion.6
  284.2 2.3 copy_dynamic-update-slice_fusion.5
  286.5 2.2 copy_dynamic-update-slice_fusion.4
  288.7 45.0 %collective-permute-done.3 = bf16[26,1,4,32,128]{4,3,2,1,0:T(8,128)(2,1)} collective-permute-done((bf16[26,1,4,32,128]{4,3,2,1,0:T(8,128)(2,1)}, bf16[26,1,4,32,128]{4,3,2,1,0:T(8,128)(2,1)}, u32[]{:S(2)}, u32[]{:S(2)}) %collective-permute-start.3) | collective-permute-done | bytes 852000 | tf_op jit(solution)/shard_map/ppermute | solution.py:21
  333.7 2.3 copy_dynamic-update-slice_fusion.3
  336.0 15.8 %collective-permute-done.4 = bf16[26,1,4,32,128]{4,3,2,1,0:T(8,128)(2,1)S(1)} collective-permute-done((bf16[26,1,4,32,128]{4,3,2,1,0:T(8,128)(2,1)S(1)}, bf16[26,1,4,32,128]{4,3,2,1,0:T(8,128)(2,1)S(1)}, u32[]{:S(2)}, u32[]{:S(2)}) %collective-permute-start.4) | collective-permute-done | bytes 852000 | tf_op jit(solution)/shard_map/ppermute | solution.py:21
  353.0 16.4 %collective-permute-done.5 = bf16[26,1,4,32,128]{4,3,2,1,0:T(8,128)(2,1)S(1)} collective-permute-done((bf16[26,1,4,32,128]{4,3,2,1,0:T(8,128)(2,1)S(1)}, bf16[26,1,4,32,128]{4,3,2,1,0:T(8,128)(2,1)S(1)}, u32[]{:S(2)}, u32[]{:S(2)}) %collective-permute-start.5) | collective-permute-done | bytes 852000 | tf_op jit(solution)/shard_map/ppermute | solution.py:21
  370.6 2.3 copy_dynamic-update-slice_fusion
  372.9 5.3 %all-to-all-start.2 = ((bf16[26,8,4,32,128]{4,3,1,0,2:T(8,128)(2,1)}), bf16[26,8,4,32,128]{4,3,1,0,2:T(8,128)(2,1)}, u32[]{:S(2)}, u32[]{:S(2)}) async-start(bf16[26,8,4,32,128]{4,3,1,0,2:T(8,128)(2,1)} %copy_dynamic-update-slice_fusion), calls=%async_computation.2 | async-start | bytes 13631488 | tf_op jit(solution)/shard_map/all_to_all | solution.py:89
  378.2 2.4 slice.25
  382.7 2.1 reshape.114
  384.9 69.6 %all-to-all-done.2 = bf16[26,8,4,32,128]{4,3,1,0,2:T(8,128)(2,1)} async-done(((bf16[26,8,4,32,128]{4,3,1,0,2:T(8,128)(2,1)}), bf16[26,8,4,32,128]{4,3,1,0,2:T(8,128)(2,1)}, u32[]{:S(2)}, u32[]{:S(2)}) %all-to-all-start.2) | async-done | bytes 6815776 | tf_op jit(solution)/shard_map/all_to_all | solution.py:89
  454.5 7.9 %copy.33 = bf16[26,8,4,32,128]{4,3,2,1,0:T(8,128)(2,1)} copy(bf16[26,8,4,32,128]{4,3,1,0,2:T(8,128)(2,1)} %all-to-all-done.2) | data formatting | bytes 13631488 | tf_op jit(solution)/shard_map/all_to_all | solution.py:89
  462.4 66.7 %while.26 = (s32[]{:T(128)}, f32[26,128,128]{2,1,0:T(8,128)}, s32[26,1024]{1,0:T(8,128)}, bf16[26,1024,128]{2,1,0:T(8,128)(2,1)}, s32[]{:T(128)}) while((s32[]{:T(128)}, f32[26,128,128]{2,1,0:T(8,128)}, s32[26,1024]{1,0:T(8,128)}, bf16[26,1024,128]{2,1,0:T(8,128)(2,1)}, s32[]{:T(128)}) %tuple.66), condition=%wide.region_6.7_spmd, body=%wide.region_5.6_spmd.sunk | while | flops 33685504 | bytes 341065 | solution.py:59
  483.7 1.8 fusion.49
  486.2 1.8 fusion.49
  504.2 1.8 fusion.49
  506.7 1.8 fusion.49
  524.7 1.8 fusion.49
  527.3 1.8 fusion.49
  (475 shorter events, 246.0 us)
Async XLA Ops:
  0.6 12.5 %copy-start = (bf16[512,27,128]{2,0,1:T(8,128)(2,1)S(1)}, bf16[512,27,128]{2,0,1:T(8,128)(2,1)}, u32[]{:S(2)}) copy-start(bf16[512,27,128]{2,0,1:T(8,128)(2,1)} %param.9) | copy-start | bytes 10616836
  17.7 3.2 copy-start.2
  194.1 10.2 %copy-start.4 = (s32[26,1024]{1,0:T(8,128)S(1)}, s32[26,1024]{1,0:T(8,128)}, u32[]{:S(2)}) copy-start(s32[26,1024]{1,0:T(8,128)} %get-tuple-element.116) | copy-start | bytes 319492
  200.8 74.9 %collective-permute-start = (bf16[26,1,4,32,128]{4,3,2,1,0:T(8,128)(2,1)}, bf16[26,1,4,32,128]{4,3,2,1,0:T(8,128)(2,1)}, u32[]{:S(2)}, u32[]{:S(2)}) collective-permute-start(bf16[26,1,4,32,128]{4,3,2,1,0:T(8,128)(2,1)} %get-tuple-element.165), channel_id=1, source_target_pairs={{0,4},{4,0},{8,12},{12,8},{16,20},{20,16},{24,28},{28,24},{1,5},{5... | collective-permute-start | bytes 2555912 | tf_op jit(solution)/shard_map/ppermute | solution.py:21
  202.3 81.9 %collective-permute-start.1 = (bf16[26,1,4,32,128]{4,3,2,1,0:T(8,128)(2,1)}, bf16[26,1,4,32,128]{4,3,2,1,0:T(8,128)(2,1)}, u32[]{:S(2)}, u32[]{:S(2)}) collective-permute-start(bf16[26,1,4,32,128]{4,3,2,1,0:T(8,128)(2,1)} %get-tuple-element.164), channel_id=1, source_target_pairs={{0,8},{4,12},{8,0},{12,4},{16,24},{20,28},{24,16},{28,20},{1,9},{5... | collective-permute-start | bytes 2555912 | tf_op jit(solution)/shard_map/ppermute | solution.py:21
  202.8 83.7 %collective-permute-start.2 = (bf16[26,1,4,32,128]{4,3,2,1,0:T(8,128)(2,1)}, bf16[26,1,4,32,128]{4,3,2,1,0:T(8,128)(2,1)}, u32[]{:S(2)}, u32[]{:S(2)}) collective-permute-start(bf16[26,1,4,32,128]{4,3,2,1,0:T(8,128)(2,1)} %get-tuple-element.163), channel_id=1, source_target_pairs={{0,12},{4,8},{8,4},{12,0},{16,28},{20,24},{24,20},{28,16},{1,13},{... | collective-permute-start | bytes 2555912 | tf_op jit(solution)/shard_map/ppermute | solution.py:21
  205.5 70.2 %copy-start.3 = (bf16[26,1,4,32,128]{4,3,2,1,0:T(8,128)(2,1)S(1)}, bf16[26,1,4,32,128]{4,3,2,1,0:T(8,128)(2,1)}, u32[]{:S(2)}) copy-start(bf16[26,1,4,32,128]{4,3,2,1,0:T(8,128)(2,1)} %get-tuple-element.161) | copy-start | bytes 2555908
  205.5 64.1 %all-to-all-start = ((s32[8,1,3328]{2,1,0:T(1,128)}), s32[8,1,3328]{2,1,0:T(1,128)S(1)}, u32[]{:S(2)}, u32[]{:S(2)}) async-start(s32[8,1,3328]{2,1,0:T(1,128)} %reshape.120), calls=%async_computation | async-start | bytes 212992 | tf_op jit(solution)/shard_map/all_to_all | solution.py:93
  211.9 158.7 %collective-permute-start.6 = (bf16[26,1,4,32,128]{4,3,2,1,0:T(8,128)(2,1)S(1)}, bf16[26,1,4,32,128]{4,3,2,1,0:T(8,128)(2,1)}, u32[]{:S(2)}, u32[]{:S(2)}) collective-permute-start(bf16[26,1,4,32,128]{4,3,2,1,0:T(8,128)(2,1)S(1)} %get-tuple-element.159), channel_id=1, source_target_pairs={{0,28},{4,24},{8,20},{12,16},{16,12},{20,8},{24,4},{28,0},{1,29},{... | collective-permute-start | bytes 2555912 | tf_op jit(solution)/shard_map/ppermute | solution.py:21
  214.3 119.4 %collective-permute-start.3 = (bf16[26,1,4,32,128]{4,3,2,1,0:T(8,128)(2,1)}, bf16[26,1,4,32,128]{4,3,2,1,0:T(8,128)(2,1)}, u32[]{:S(2)}, u32[]{:S(2)}) collective-permute-start(bf16[26,1,4,32,128]{4,3,2,1,0:T(8,128)(2,1)} %get-tuple-element.162), channel_id=1, source_target_pairs={{0,16},{4,20},{8,24},{12,28},{16,0},{20,4},{24,8},{28,12},{1,17},{... | collective-permute-start | bytes 2555912 | tf_op jit(solution)/shard_map/ppermute | solution.py:21
  272.4 100.5 %all-to-all-start.1 = ((s32[4,1,6656]{2,1,0:T(1,128)}), s32[4,1,6656]{2,1,0:T(1,128)S(1)}, u32[]{:S(2)}, u32[]{:S(2)}) async-start(s32[4,1,6656]{2,1,0:T(1,128)} %reshape.122), calls=%async_computation.1 | async-start | bytes 212992 | tf_op jit(solution)/shard_map/all_to_all | solution.py:92
  275.7 76.1 %collective-permute-start.4 = (bf16[26,1,4,32,128]{4,3,2,1,0:T(8,128)(2,1)S(1)}, bf16[26,1,4,32,128]{4,3,2,1,0:T(8,128)(2,1)S(1)}, u32[]{:S(2)}, u32[]{:S(2)}) collective-permute-start(bf16[26,1,4,32,128]{4,3,2,1,0:T(8,128)(2,1)S(1)} %copy-done.3), channel_id=1, source_target_pairs={{0,20},{4,16},{8,28},{12,24},{16,4},{20,0},{24,12},{28,8},{1,21},{... | collective-permute-start | bytes 2555912 | tf_op jit(solution)/shard_map/ppermute | solution.py:21
  284.2 85.2 %collective-permute-start.5 = (bf16[26,1,4,32,128]{4,3,2,1,0:T(8,128)(2,1)S(1)}, bf16[26,1,4,32,128]{4,3,2,1,0:T(8,128)(2,1)S(1)}, u32[]{:S(2)}, u32[]{:S(2)}) collective-permute-start(bf16[26,1,4,32,128]{4,3,2,1,0:T(8,128)(2,1)S(1)} %get-tuple-element.160), channel_id=1, source_target_pairs={{0,24},{4,28},{8,16},{12,20},{16,8},{20,12},{24,0},{28,4},{1,25},{... | collective-permute-start | bytes 2555912 | tf_op jit(solution)/shard_map/ppermute | solution.py:21
  372.9 81.6 %all-to-all-start.2 = ((bf16[26,8,4,32,128]{4,3,1,0,2:T(8,128)(2,1)}), bf16[26,8,4,32,128]{4,3,1,0,2:T(8,128)(2,1)}, u32[]{:S(2)}, u32[]{:S(2)}) async-start(bf16[26,8,4,32,128]{4,3,1,0,2:T(8,128)(2,1)} %copy_dynamic-update-slice_fusion), calls=%async_computation.2 | async-start | bytes 13631488 | tf_op jit(solution)/shard_map/all_to_all | solution.py:89
  382.7 146.4 %copy-start.1 = (bf16[512,27,128]{2,0,1:T(8,128)(2,1)S(1)}, bf16[512,27,128]{2,0,1:T(8,128)(2,1)}, u32[]{:S(2)}) copy-start(bf16[512,27,128]{2,0,1:T(8,128)(2,1)} %param.9) | copy-start | bytes 10616836
